TPU v7x, 32 devices: a whole 2x2x4 slice. The times are simulated.
32 devices in a mesh: image: 2 (over x), band: 16 (over z, y, core).
Axes of the slice: x: 2, y: 2, z: 4, core: 2. Of those that a mesh axis runs over, the one named last changes fastest.
Arguments:
- orbitals: bfloat16 [32, 64, 4096], P(('image', 'band')), parts along dimension 0, may hold values from -6 to 6
- kernel: float32 [128, 4096], P('image'), parts along dimension 0, may hold values from 0.05 to 1
Outputs:
- exchange: bfloat16 [32, 64, 4096], P(('image', 'band')), parts along dimension 0
- energy: float32 [2], P('image'), parts along dimension 0
There are 2 independent parts, one for each index of `image`. A program takes and returns all parts, laid end to end along the dimension named above; each array names one. Nothing has to cross between parts.
All inputs are finite; a program needn't handle non-finite values.
Results may differ from a plain program's by a relative error of at most 0.009.
Values may be sent and summed in bfloat16 or wider, within the bound.
A program may use at most 64 MiB of HBM per device.

v0:
```python
import functools

import jax
import jax.numpy as jnp
import numpy as np
from jax import lax
from jax.experimental import pallas as pl
from jax.experimental.pallas import tpu as pltpu
from jax.sharding import PartitionSpec as P

MESH = pl.DeviceIdType.MESH
F32 = jnp.float32
BF16 = jnp.bfloat16


def cas_table(length):
    wave_index = np.arange(length, dtype=np.int32)
    phase_index = wave_index[:, None] * wave_index[None, :] % length
    angles = phase_index.astype(np.float32) * np.float32(2.0 * np.pi / length)
    table = (np.cos(angles) + np.sin(angles)) / np.float32(np.sqrt(length))
    return table.astype(np.float32)


def dot(a, b):
    return jnp.dot(a, b, preferred_element_type=F32)


def split_halves(low, high, g):
    lane = lax.broadcasted_iota(jnp.int32, low.shape, 1)
    first = jnp.concatenate([low[:, :g], high[:, :g]], axis=1)
    second = jnp.concatenate([low[:, g:], high[:, g:]], axis=1)
    del lane
    return first, second


def kernel(n, g, orb, vin, hx, hy, out, en, slots, vdup, mdup, pack, t1, t2, acc,
           e_own, e_all, send_sem, recv_sem, e_send, e_recv):
    me = lax.axis_index("band")
    odd = lax.rem(me, 2)
    at = lambda d: lax.rem(me + d + n, n)
    partner = at(1 - 2 * odd)
    up, down = at(2), at(-2)
    far = at(6 * odd - 3)
    to = lambda b: {"band": b}

    barrier = pltpu.get_barrier_semaphore()

    @pl.loop(1, n)
    def _(d):
        pl.semaphore_signal(barrier, inc=1, device_id=to(lax.rem(me + d, n)), device_id_type=MESH)

    pl.semaphore_wait(barrier, n - 1)

    def copy(k, src, dst):
        return pltpu.make_async_remote_copy(
            src_ref=src, dst_ref=slots.at[k], send_sem=send_sem.at[k], recv_sem=recv_sem.at[k],
            device_id=to(dst), device_id_type=MESH)

    copies = [copy(0, orb, partner), copy(1, orb, up), copy(2, orb, down), copy(3, orb, far),
              copy(4, slots.at[1], partner), copy(5, slots.at[2], partner)]
    for k in (1, 2, 3, 0):
        copies[k].start()

    half = g // 2
    xh_n = g // 8

    @pl.loop(0, half)
    def _(t):
        c = pl.ds(pl.multiple_of(t * 2 * g, 2 * g), 2 * g)
        m = orb[:, c]
        a, b = split_halves(m, m, g)
        mdup[2 * t] = a
        mdup[2 * t + 1] = b
        v = vin[:, c]
        a, b = split_halves(v, v, g)
        for xh in range(xh_n):
            r = slice(xh * 8, xh * 8 + 8)
            vdup[xh, pl.ds(pl.multiple_of(t * 16, 16), 8), :] = a[r]
            vdup[xh, pl.ds(pl.multiple_of(t * 16 + 8, 8), 8), :] = b[r]

    def tiles(ref, yg):
        parts = [ref[pl.ds(yg * 8 + ya * 4, 4)].reshape(4 * g, 2 * g) for ya in range(2)]
        return jnp.concatenate(parts, axis=1)

    def group(a_ref, b_ref, first):
        @pl.loop(0, half)
        def _(t):
            c = pl.ds(pl.multiple_of(t * 2 * g, 2 * g), 2 * g)
            a = a_ref[:, c]
            b = jnp.zeros_like(a) if b_ref is None else b_ref[:, c]
            p, q = split_halves(a, b, g)
            pack[2 * t] = p
            pack[2 * t + 1] = q

        @pl.loop(0, g // 8, unroll=2)
        def _(yg):
            d = tiles(mdup, yg) * tiles(pack, yg)
            h = hx[...]
            u = dot(h, d).astype(BF16)
            u = dot(u, h).reshape(4, xh_n, 8, 4 * g)
            for xh in range(xh_n):
                for ya in range(2):
                    piece = u[:, xh, :, ya * 2 * g:(ya + 1) * 2 * g].reshape(32, 2 * g)
                    rows = pl.ds(pl.multiple_of(yg * 64 + ya * 32, 32), 32)
                    t1[xh, rows, :] = piece.astype(BF16)

        @pl.loop(0, xh_n // 2)
        def _(xg):
            w = jnp.concatenate([t1[2 * xg], t1[2 * xg + 1]], axis=1)
            v = jnp.concatenate([vdup[2 * xg], vdup[2 * xg + 1]], axis=1)
            k = hy[...]
            w = (dot(k, w) * v).astype(BF16)
            w = dot(k, w).reshape(g, 8, 4 * g)
            w = jnp.concatenate([w[:, :, :2 * g], w[:, :, 2 * g:]], axis=1)
            t2[:, pl.ds(pl.multiple_of(xg * 16, 16), 16), :] = w.astype(BF16)

        @pl.loop(0, g // 8, unroll=2)
        def _(yg):
            h = hx[...]
            u = dot(tiles(t2, yg), h).astype(BF16)
            u = dot(h, u) * tiles(pack, yg).astype(F32)
            for ya in range(2):
                y = pl.ds(yg * 8 + ya * 4, 4)
                piece = u[:, ya * 2 * g:(ya + 1) * 2 * g].reshape(4, g, 2 * g)
                acc[y] = piece if first else acc[y] + piece

    copies[0].wait_recv()
    group(orb, slots.at[0], True)
    copies[1].wait_recv()
    copies[4].start()
    copies[2].wait_recv()
    copies[5].start()
    group(slots.at[1], slots.at[2], False)
    copies[4].wait_recv()
    copies[5].wait_recv()
    group(slots.at[4], slots.at[5], False)
    copies[3].wait_recv()
    group(slots.at[3], None, False)

    e_own[...] = jnp.zeros_like(e_own)

    @pl.loop(0, half)
    def _(t):
        c = pl.ds(pl.multiple_of(t * 2 * g, 2 * g), 2 * g)
        e = acc[2 * t]
        o = acc[2 * t + 1]
        total = -jnp.concatenate([e[:, :g] + e[:, g:], o[:, :g] + o[:, g:]], axis=1)
        out[:, c] = total.astype(BF16)
        s = total * orb[:, c].astype(F32)
        e_own[...] += jnp.sum(s.reshape(g // 8, 8, 2 * g), axis=0)

    def share(d):
        there = lax.rem(me + d, n)
        return pltpu.make_async_remote_copy(
            src_ref=e_own, dst_ref=e_all.at[d], send_sem=e_send.at[d], recv_sem=e_recv.at[d],
            device_id=to(there), device_id_type=MESH)

    @pl.loop(1, n)
    def _(d):
        share(d).start()

    for k in range(6):
        copies[k].wait_send()

    e_all[0] = e_own[...]

    @pl.loop(1, n)
    def _(d):
        share(d).wait()

    en[0] = 0.5 * jnp.sum(jnp.sum(e_all[...], axis=0)) / float(g ** 3)


def shards(orbitals, weights):
    _, g, area = orbitals.shape
    n = lax.axis_size("band")
    table = cas_table(g)
    hx = jnp.asarray(np.kron(np.eye(4, dtype=np.float32), table), BF16)
    hy = jnp.asarray(np.kron(table, np.eye(8, dtype=np.float32)), BF16)
    vm = pl.BlockSpec(memory_space=pltpu.VMEM)
    exchange, energy = pl.pallas_call(
        functools.partial(kernel, n, g),
        out_shape=(jax.ShapeDtypeStruct((g, area), BF16), jax.ShapeDtypeStruct((1,), F32)),
        in_specs=[vm] * 4,
        out_specs=(vm, pl.BlockSpec(memory_space=pltpu.SMEM)),
        scratch_shapes=[
            pltpu.VMEM((6, g, area), BF16),
            pltpu.VMEM((g // 8, 8 * g, 2 * g), F32),
            pltpu.VMEM((g, g, 2 * g), BF16),
            pltpu.VMEM((g, g, 2 * g), BF16),
            pltpu.VMEM((g // 8, 8 * g, 2 * g), BF16),
            pltpu.VMEM((g, g, 2 * g), BF16),
            pltpu.VMEM((g, g, 2 * g), F32),
            pltpu.VMEM((8, 2 * g), F32),
            pltpu.VMEM((n, 8, 2 * g), F32),
            pltpu.SemaphoreType.DMA((6,)),
            pltpu.SemaphoreType.DMA((6,)),
            pltpu.SemaphoreType.DMA((n,)),
            pltpu.SemaphoreType.DMA((n,)),
        ],
        compiler_params=pltpu.CompilerParams(
            collective_id=0, has_side_effects=True, vmem_limit_bytes=48 * 1024 * 1024),
    )(orbitals.reshape(g, area), weights, hx, hy)
    return exchange.reshape(orbitals.shape), energy


def solution(mesh):
    in_specs = (P(("image", "band"), None, None), P("image", None))
    out_specs = (P(("image", "band"), None, None), P("image"))
    return jax.shard_map(shards, mesh=mesh, in_specs=in_specs, out_specs=out_specs, check_vma=False)
```

profile of v0, /device:TPU:0, one launch (start us, length us, event | category | flops | bytes accessed | tf_op | source)
XLA Modules:
  0.0 73.9 jit_solution(10604349384851060516)
XLA Ops:
  0.6 0.0 copy-start
  0.6 1.2 %copy-done = f32[64,4096]{1,0:T(8,128)S(1)} copy-done((f32[64,4096]{1,0:T(8,128)S(1)}, f32[64,4096]{1,0:T(8,128)}, u32[]{:S(2)}) %copy-start) | copy-done | bytes 1048600
  1.9 0.0 copy-start.1
  1.9 1.0 %copy-done.1 = bf16[1,64,4096]{2,1,0:T(8,128)(2,1)S(1)} copy-done((bf16[1,64,4096]{2,1,0:T(8,128)(2,1)S(1)}, bf16[1,64,4096]{2,1,0:T(8,128)(2,1)}, u32[]{:S(2)}) %copy-start.1) | copy-done | bytes 524312
  2.9 0.0 copy-start.2
  2.9 1.0 %copy-done.2 = bf16[512,512]{1,0:T(8,128)(2,1)S(1)} copy-done((bf16[512,512]{1,0:T(8,128)(2,1)S(1)}, bf16[512,512]{1,0:T(8,128)(2,1)}, u32[]{:S(2)}) %copy-start.2) | copy-done | bytes 524312
  3.9 0.0 copy-start.3
  3.9 0.9 %copy-done.3 = bf16[256,256]{1,0:T(8,128)(2,1)S(1)} copy-done((bf16[256,256]{1,0:T(8,128)(2,1)S(1)}, bf16[256,256]{1,0:T(8,128)(2,1)}, u32[]{:S(2)}) %copy-start.3) | copy-done | bytes 131096
  4.8 66.5 %shard_map.59 = (bf16[64,4096]{1,0:T(8,128)(2,1)S(1)}, f32[1]{0:T(128)}) custom-call(bf16[64,4096]{1,0:T(8,128)(2,1)S(1)} %bitcast.2, f32[64,4096]{1,0:T(8,128)S(1)} %copy-done, bf16[256,256]{1,0:T(8,128)(2,1)S(1)} %copy-done.3, bf16[512,512]{1,0:T(8,128)(2,1)S(1)} %copy-done.2), custom_call_target="tpu_custom_call" | custom-call | tf_op jit(solution)/shard_map/pallas_call | solution.py:181
  71.3 0.8 %copy.8 = bf16[1,64,4096]{2,1,0:T(8,128)(2,1)} copy(bf16[1,64,4096]{2,1,0:T(8,128)(2,1)S(1)} %bitcast.3) | data formatting | bytes 1048576
Async XLA Ops:
  0.6 1.2 %copy-start = (f32[64,4096]{1,0:T(8,128)S(1)}, f32[64,4096]{1,0:T(8,128)}, u32[]{:S(2)}) copy-start(f32[64,4096]{1,0:T(8,128)} %vin.1) | copy-start | bytes 3145732
  1.9 1.0 %copy-start.1 = (bf16[1,64,4096]{2,1,0:T(8,128)(2,1)S(1)}, bf16[1,64,4096]{2,1,0:T(8,128)(2,1)}, u32[]{:S(2)}) copy-start(bf16[1,64,4096]{2,1,0:T(8,128)(2,1)} %param.4) | copy-start | bytes 1572868
  2.9 1.0 %copy-start.2 = (bf16[512,512]{1,0:T(8,128)(2,1)S(1)}, bf16[512,512]{1,0:T(8,128)(2,1)}, u32[]{:S(2)}) copy-start(bf16[512,512]{1,0:T(8,128)(2,1)} %constant.5.clone.hy) | copy-start | bytes 1572868
  3.9 0.9 %copy-start.3 = (bf16[256,256]{1,0:T(8,128)(2,1)S(1)}, bf16[256,256]{1,0:T(8,128)(2,1)}, u32[]{:S(2)}) copy-start(bf16[256,256]{1,0:T(8,128)(2,1)} %constant.4.clone.hx) | copy-start | bytes 393220
where the time goes:
time: 74.2 us; the launch traced here: 73.9 us
  Pallas kernels  66.5 us (90%)
  local copies, waits for them, and re-layouts  5 us (7%)
  between operations  2.4 us (3%)
    pallas_call x1, Pallas kernels, shards(): pl.pallas_call(functools.partial(kernel, n, g), out_shape=(jax.ShapeDtype...  66.5 us
    unnamed x9, local copies, waits for them, and re-layouts  5 us

commit v1 on v0

--- a/solution.py
+++ b/solution.py
@@ -8,6 +8,7 @@
 from jax.experimental.pallas import tpu as pltpu
 from jax.sharding import PartitionSpec as P
 
+CHUNKS = 4
 MESH = pl.DeviceIdType.MESH
 F32 = jnp.float32
 BF16 = jnp.bfloat16
@@ -26,22 +27,27 @@
 
 
 def split_halves(low, high, g):
-    lane = lax.broadcasted_iota(jnp.int32, low.shape, 1)
     first = jnp.concatenate([low[:, :g], high[:, :g]], axis=1)
     second = jnp.concatenate([low[:, g:], high[:, g:]], axis=1)
-    del lane
     return first, second
 
 
-def kernel(n, g, orb, vin, hx, hy, out, en, slots, vdup, mdup, pack, t1, t2, acc,
-           e_own, e_all, send_sem, recv_sem, e_send, e_recv):
+def kernel(n, g, orb_hbm, vin_hbm, hx_hbm, hy_hbm, out, en, orb, vin, hx, hy, slots, vdup, mdup,
+           pack, t1, t2, acc, e_own, e_all, in_sem, send_sem, recv_sem, e_send, e_recv):
     me = lax.axis_index("band")
-    odd = lax.rem(me, 2)
+    core = lax.rem(me, 2)
+    side = 1 - 2 * lax.rem(me // 2, 2)
     at = lambda d: lax.rem(me + d + n, n)
-    partner = at(1 - 2 * odd)
-    up, down = at(2), at(-2)
-    far = at(6 * odd - 3)
+    partner = at(1 - 2 * core)
+    near = at(2 * side)
+    beyond = at(4 * side)
+    far = at(6 * core - 3)
     to = lambda b: {"band": b}
+
+    loads = [pltpu.make_async_copy(src, dst, in_sem.at[i]) for i, (src, dst) in enumerate(
+        ((orb_hbm, orb), (vin_hbm, vin), (hx_hbm, hx), (hy_hbm, hy)))]
+    for load in loads:
+        load.start()
 
     barrier = pltpu.get_barrier_semaphore()
 
@@ -49,22 +55,47 @@
     def _(d):
         pl.semaphore_signal(barrier, inc=1, device_id=to(lax.rem(me + d, n)), device_id_type=MESH)
 
+    loads[0].wait()
     pl.semaphore_wait(barrier, n - 1)
 
-    def copy(k, src, dst):
-        return pltpu.make_async_remote_copy(
-            src_ref=src, dst_ref=slots.at[k], send_sem=send_sem.at[k], recv_sem=recv_sem.at[k],
-            device_id=to(dst), device_id_type=MESH)
-
-    copies = [copy(0, orb, partner), copy(1, orb, up), copy(2, orb, down), copy(3, orb, far),
-              copy(4, slots.at[1], partner), copy(5, slots.at[2], partner)]
-    for k in (1, 2, 3, 0):
-        copies[k].start()
+    rows = g // CHUNKS
+
+    def copies(k, src, dst):
+        return [pltpu.make_async_remote_copy(
+            src_ref=src.at[pl.ds(i * rows, rows)], dst_ref=slots.at[k, pl.ds(i * rows, rows)],
+            send_sem=send_sem.at[k, i], recv_sem=recv_sem.at[k, i],
+            device_id=to(dst), device_id_type=MESH) for i in range(CHUNKS)]
+
+    to_partner = copies(0, orb, partner)
+    to_near = copies(1, orb, near)
+    relayed = copies(2, slots.at[1], beyond)
+    to_far = copies(3, orb, far)
+    pass_near = copies(4, slots.at[1], partner)
+    pass_relayed = copies(5, slots.at[2], partner)
+    for group_of in (to_near, to_far, to_partner):
+        for c in group_of:
+            c.start()
+
+    def relay_near(i):
+        to_near[i].wait_recv()
+        relayed[i].start()
+        pass_near[i].start()
+
+    def relay_far(i):
+        relayed[i].wait_recv()
+        pass_relayed[i].start()
+
+    def arrived(group_of):
+        for c in group_of:
+            c.wait_recv()
+
+    for load in loads[1:]:
+        load.wait()
 
     half = g // 2
     xh_n = g // 8
 
-    @pl.loop(0, half)
+    @pl.loop(0, half, unroll=8)
     def _(t):
         c = pl.ds(pl.multiple_of(t * 2 * g, 2 * g), 2 * g)
         m = orb[:, c]
@@ -82,8 +113,8 @@
         parts = [ref[pl.ds(yg * 8 + ya * 4, 4)].reshape(4 * g, 2 * g) for ya in range(2)]
         return jnp.concatenate(parts, axis=1)
 
-    def group(a_ref, b_ref, first):
-        @pl.loop(0, half)
+    def group(a_ref, b_ref, first, hook1, hook2):
+        @pl.loop(0, half, unroll=8)
         def _(t):
             c = pl.ds(pl.multiple_of(t * 2 * g, 2 * g), 2 * g)
             a = a_ref[:, c]
@@ -92,7 +123,7 @@
             pack[2 * t] = p
             pack[2 * t + 1] = q
 
-        @pl.loop(0, g // 8, unroll=2)
+        @pl.loop(0, g // 8, unroll=8)
         def _(yg):
             d = tiles(mdup, yg) * tiles(pack, yg)
             h = hx[...]
@@ -104,7 +135,9 @@
                     rows = pl.ds(pl.multiple_of(yg * 64 + ya * 32, 32), 32)
                     t1[xh, rows, :] = piece.astype(BF16)
 
-        @pl.loop(0, xh_n // 2)
+        hook1()
+
+        @pl.loop(0, xh_n // 2, unroll=4)
         def _(xg):
             w = jnp.concatenate([t1[2 * xg], t1[2 * xg + 1]], axis=1)
             v = jnp.concatenate([vdup[2 * xg], vdup[2 * xg + 1]], axis=1)
@@ -114,7 +147,9 @@
             w = jnp.concatenate([w[:, :, :2 * g], w[:, :, 2 * g:]], axis=1)
             t2[:, pl.ds(pl.multiple_of(xg * 16, 16), 16), :] = w.astype(BF16)
 
-        @pl.loop(0, g // 8, unroll=2)
+        hook2()
+
+        @pl.loop(0, g // 8, unroll=8)
         def _(yg):
             h = hx[...]
             u = dot(tiles(t2, yg), h).astype(BF16)
@@ -124,22 +159,21 @@
                 piece = u[:, ya * 2 * g:(ya + 1) * 2 * g].reshape(4, g, 2 * g)
                 acc[y] = piece if first else acc[y] + piece
 
-    copies[0].wait_recv()
-    group(orb, slots.at[0], True)
-    copies[1].wait_recv()
-    copies[4].start()
-    copies[2].wait_recv()
-    copies[5].start()
-    group(slots.at[1], slots.at[2], False)
-    copies[4].wait_recv()
-    copies[5].wait_recv()
-    group(slots.at[4], slots.at[5], False)
-    copies[3].wait_recv()
-    group(slots.at[3], None, False)
+    arrived(to_partner)
+    group(orb, slots.at[0], True, lambda: relay_near(0), lambda: relay_near(1))
+    arrived(to_far)
+    group(slots.at[3], None, False, lambda: relay_near(2), lambda: None)
+    relay_near(3)
+    arrived(pass_near)
+    group(slots.at[1], slots.at[4], False, lambda: relay_far(0), lambda: relay_far(1))
+    relay_far(2)
+    relay_far(3)
+    arrived(pass_relayed)
+    group(slots.at[2], slots.at[5], False, lambda: None, lambda: None)
 
     e_own[...] = jnp.zeros_like(e_own)
 
-    @pl.loop(0, half)
+    @pl.loop(0, half, unroll=8)
     def _(t):
         c = pl.ds(pl.multiple_of(t * 2 * g, 2 * g), 2 * g)
         e = acc[2 * t]
@@ -159,8 +193,9 @@
     def _(d):
         share(d).start()
 
-    for k in range(6):
-        copies[k].wait_send()
+    for group_of in (to_partner, to_near, relayed, to_far, pass_near, pass_relayed):
+        for c in group_of:
+            c.wait_send()
 
     e_all[0] = e_own[...]
 
@@ -181,9 +216,13 @@
     exchange, energy = pl.pallas_call(
         functools.partial(kernel, n, g),
         out_shape=(jax.ShapeDtypeStruct((g, area), BF16), jax.ShapeDtypeStruct((1,), F32)),
-        in_specs=[vm] * 4,
+        in_specs=[pl.BlockSpec(memory_space=pl.ANY)] * 4,
         out_specs=(vm, pl.BlockSpec(memory_space=pltpu.SMEM)),
         scratch_shapes=[
+            pltpu.VMEM((g, area), BF16),
+            pltpu.VMEM((g, area), F32),
+            pltpu.VMEM(hx.shape, BF16),
+            pltpu.VMEM(hy.shape, BF16),
             pltpu.VMEM((6, g, area), BF16),
             pltpu.VMEM((g // 8, 8 * g, 2 * g), F32),
             pltpu.VMEM((g, g, 2 * g), BF16),
@@ -193,13 +232,14 @@
             pltpu.VMEM((g, g, 2 * g), F32),
             pltpu.VMEM((8, 2 * g), F32),
             pltpu.VMEM((n, 8, 2 * g), F32),
-            pltpu.SemaphoreType.DMA((6,)),
-            pltpu.SemaphoreType.DMA((6,)),
+            pltpu.SemaphoreType.DMA((4,)),
+            pltpu.SemaphoreType.DMA((6, CHUNKS)),
+            pltpu.SemaphoreType.DMA((6, CHUNKS)),
             pltpu.SemaphoreType.DMA((n,)),
             pltpu.SemaphoreType.DMA((n,)),
         ],
         compiler_params=pltpu.CompilerParams(
-            collective_id=0, has_side_effects=True, vmem_limit_bytes=48 * 1024 * 1024),
+            collective_id=0, has_side_effects=True, vmem_limit_bytes=60 * 1024 * 1024),
     )(orbitals.reshape(g, area), weights, hx, hy)
     return exchange.reshape(orbitals.shape), energy
 

time: 74.2 us -> 46.9 us (0.63)
  Pallas kernels: 66.5 us -> 42.5 us
  local copies, waits for them, and re-layouts: 5 us -> 1.87 us
    pallas_call x1, Pallas kernels: 66.5 us -> 42.5 us  [shards(): pl.pallas_call(functools.partial(kernel, n, g), out_shape=(jax.ShapeDtype...]
    unnamed x9 -> x1, local copies, waits for them, and re-layouts: 5 us -> 1.87 us
where the time goes in v1:
time: 46.9 us; the launch traced here: 46.7 us
  Pallas kernels  42.5 us (91%)
  between operations  2.33 us (5%)
  local copies, waits for them, and re-layouts  1.87 us (4%)
    pallas_call x1, Pallas kernels, shards(): pl.pallas_call(functools.partial(kernel, n, g), out_shape=(jax.ShapeDtype...  42.5 us
    unnamed x1, local copies, waits for them, and re-layouts  1.87 us

profile of v1, /device:TPU:0, one launch (start us, length us, event | category | flops | bytes accessed | tf_op | source)
XLA Modules:
  0.0 46.7 jit_solution(17767087525589820574)
XLA Ops:
  0.6 42.5 %shard_map.59 = (bf16[64,4096]{1,0:T(8,128)(2,1)}, f32[1]{0:T(128)}) custom-call(bf16[64,4096]{1,0:T(8,128)(2,1)} %bitcast.2, f32[64,4096]{1,0:T(8,128)} %vin_hbm.1, bf16[256,256]{1,0:T(8,128)(2,1)} %constant.4.clone.hx_hbm, bf16[512,512]{1,0:T(8,128)(2,1)} %constant.5.clone.hy_hbm), custom_call_target="tpu_custom_call" | custom-call | tf_op jit(solution)/shard_map/pallas_call | solution.py:216
  43.2 1.9 %copy.8 = bf16[1,64,4096]{2,1,0:T(8,128)(2,1)} copy(bf16[1,64,4096]{2,1,0:T(8,128)(2,1)} %bitcast.3) | data formatting | bytes 1048576

commit v2 on v1

--- a/solution.py
+++ b/solution.py
@@ -41,7 +41,8 @@
     partner = at(1 - 2 * core)
     near = at(2 * side)
     beyond = at(4 * side)
-    far = at(6 * core - 3)
+    far, beside = at(3 * side), at(side)
+    sends_far = lax.rem(core + lax.rem(me // 2, 2), 2) == 1
     to = lambda b: {"band": b}
 
     loads = [pltpu.make_async_copy(src, dst, in_sem.at[i]) for i, (src, dst) in enumerate(
@@ -58,36 +59,50 @@
     loads[0].wait()
     pl.semaphore_wait(barrier, n - 1)
 
-    rows = g // CHUNKS
-
-    def copies(k, src, dst):
+    wide = g * g // CHUNKS
+
+    def copies(k, src, dst, send):
+        columns = [pl.ds(i * wide, wide) for i in range(CHUNKS)]
         return [pltpu.make_async_remote_copy(
-            src_ref=src.at[pl.ds(i * rows, rows)], dst_ref=slots.at[k, pl.ds(i * rows, rows)],
-            send_sem=send_sem.at[k, i], recv_sem=recv_sem.at[k, i],
-            device_id=to(dst), device_id_type=MESH) for i in range(CHUNKS)]
-
-    to_partner = copies(0, orb, partner)
-    to_near = copies(1, orb, near)
-    relayed = copies(2, slots.at[1], beyond)
-    to_far = copies(3, orb, far)
-    pass_near = copies(4, slots.at[1], partner)
-    pass_relayed = copies(5, slots.at[2], partner)
-    for group_of in (to_near, to_far, to_partner):
-        for c in group_of:
+            src_ref=src.at[:, c], dst_ref=slots.at[k, :, c],
+            send_sem=send_sem.at[send, i], recv_sem=recv_sem.at[k, i],
+            device_id=to(dst), device_id_type=MESH) for i, c in enumerate(columns)]
+
+    to_partner = copies(0, orb, partner, 0)
+    to_near = copies(1, orb, near, 1)
+    relayed = copies(2, slots.at[1], beyond, 2)
+    to_far = copies(3, orb, far, 3)
+    pass_near = copies(4, slots.at[1], partner, 4)
+    pass_relayed = copies(5, slots.at[2], partner, 5)
+    to_beside = copies(3, slots.at[2], beside, 6)
+
+    for c in to_near:
+        c.start()
+
+    @pl.when(sends_far)
+    def _():
+        for c in to_far[:2]:
             c.start()
+
+    for c in to_partner:
+        c.start()
 
     def relay_near(i):
         to_near[i].wait_recv()
         relayed[i].start()
         pass_near[i].start()
+        if i >= 2:
+            @pl.when(sends_far)
+            def _():
+                to_far[i].start()
 
     def relay_far(i):
         relayed[i].wait_recv()
         pass_relayed[i].start()
 
-    def arrived(group_of):
-        for c in group_of:
-            c.wait_recv()
+        @pl.when(sends_far)
+        def _():
+            to_beside[i].start()
 
     for load in loads[1:]:
         load.wait()
@@ -113,27 +128,30 @@
         parts = [ref[pl.ds(yg * 8 + ya * 4, 4)].reshape(4 * g, 2 * g) for ya in range(2)]
         return jnp.concatenate(parts, axis=1)
 
-    def group(a_ref, b_ref, first, hook1, hook2):
-        @pl.loop(0, half, unroll=8)
-        def _(t):
-            c = pl.ds(pl.multiple_of(t * 2 * g, 2 * g), 2 * g)
-            a = a_ref[:, c]
-            b = jnp.zeros_like(a) if b_ref is None else b_ref[:, c]
-            p, q = split_halves(a, b, g)
-            pack[2 * t] = p
-            pack[2 * t + 1] = q
-
-        @pl.loop(0, g // 8, unroll=8)
-        def _(yg):
-            d = tiles(mdup, yg) * tiles(pack, yg)
-            h = hx[...]
-            u = dot(h, d).astype(BF16)
-            u = dot(u, h).reshape(4, xh_n, 8, 4 * g)
-            for xh in range(xh_n):
-                for ya in range(2):
-                    piece = u[:, xh, :, ya * 2 * g:(ya + 1) * 2 * g].reshape(32, 2 * g)
-                    rows = pl.ds(pl.multiple_of(yg * 64 + ya * 32, 32), 32)
-                    t1[xh, rows, :] = piece.astype(BF16)
+    def group(a_ref, b_ref, first, ready, hook1, hook2):
+        for i in range(CHUNKS):
+            ready(i)
+
+            @pl.loop(i * half // CHUNKS, (i + 1) * half // CHUNKS, unroll=half // CHUNKS)
+            def _(t):
+                c = pl.ds(pl.multiple_of(t * 2 * g, 2 * g), 2 * g)
+                a = a_ref[:, c]
+                b = jnp.zeros_like(a) if b_ref is None else b_ref[:, c]
+                p, q = split_halves(a, b, g)
+                pack[2 * t] = p
+                pack[2 * t + 1] = q
+
+            @pl.loop(i * g // 8 // CHUNKS, (i + 1) * g // 8 // CHUNKS, unroll=g // 8 // CHUNKS)
+            def _(yg):
+                d = tiles(mdup, yg) * tiles(pack, yg)
+                h = hx[...]
+                u = dot(h, d).astype(BF16)
+                u = dot(u, h).reshape(4, xh_n, 8, 4 * g)
+                for xh in range(xh_n):
+                    for ya in range(2):
+                        piece = u[:, xh, :, ya * 2 * g:(ya + 1) * 2 * g].reshape(32, 2 * g)
+                        rows = pl.ds(pl.multiple_of(yg * 64 + ya * 32, 32), 32)
+                        t1[xh, rows, :] = piece.astype(BF16)
 
         hook1()
 
@@ -159,17 +177,25 @@
                 piece = u[:, ya * 2 * g:(ya + 1) * 2 * g].reshape(4, g, 2 * g)
                 acc[y] = piece if first else acc[y] + piece
 
-    arrived(to_partner)
-    group(orb, slots.at[0], True, lambda: relay_near(0), lambda: relay_near(1))
-    arrived(to_far)
-    group(slots.at[3], None, False, lambda: relay_near(2), lambda: None)
-    relay_near(3)
-    arrived(pass_near)
-    group(slots.at[1], slots.at[4], False, lambda: relay_far(0), lambda: relay_far(1))
-    relay_far(2)
-    relay_far(3)
-    arrived(pass_relayed)
-    group(slots.at[2], slots.at[5], False, lambda: None, lambda: None)
+    def ready_near(i):
+        if i >= 2:
+            relay_near(i)
+        pass_near[i].wait_recv()
+
+    def ready_relayed(i):
+        if i >= 3:
+            relay_far(i)
+        pass_relayed[i].wait_recv()
+
+    def far_hook():
+        relay_far(0)
+        relay_far(1)
+
+    group(orb, slots.at[0], True, lambda i: to_partner[i].wait_recv(),
+          lambda: relay_near(0), lambda: relay_near(1))
+    group(slots.at[1], slots.at[4], False, ready_near, far_hook, lambda: relay_far(2))
+    group(slots.at[2], slots.at[5], False, ready_relayed, lambda: None, lambda: None)
+    group(slots.at[3], None, False, lambda i: to_far[i].wait_recv(), lambda: None, lambda: None)
 
     e_own[...] = jnp.zeros_like(e_own)
 
@@ -193,8 +219,13 @@
     def _(d):
         share(d).start()
 
-    for group_of in (to_partner, to_near, relayed, to_far, pass_near, pass_relayed):
-        for c in group_of:
+    for sent in (to_partner, to_near, relayed, pass_near, pass_relayed):
+        for c in sent:
+            c.wait_send()
+
+    @pl.when(sends_far)
+    def _():
+        for c in to_far + to_beside:
             c.wait_send()
 
     e_all[0] = e_own[...]
@@ -233,7 +264,7 @@
             pltpu.VMEM((8, 2 * g), F32),
             pltpu.VMEM((n, 8, 2 * g), F32),
             pltpu.SemaphoreType.DMA((4,)),
-            pltpu.SemaphoreType.DMA((6, CHUNKS)),
+            pltpu.SemaphoreType.DMA((7, CHUNKS)),
             pltpu.SemaphoreType.DMA((6, CHUNKS)),
             pltpu.SemaphoreType.DMA((n,)),
             pltpu.SemaphoreType.DMA((n,)),

time: 46.9 us -> 45.2 us (0.964)
  Pallas kernels: 42.5 us -> 40.7 us
    pallas_call x1, Pallas kernels: 42.5 us -> 40.7 us  [shards(): pl.pallas_call(functools.partial(kernel, n, g), out_shape=(jax.ShapeDtype...]
where the time goes in v2:
time: 45.2 us; the launch traced here: 45 us
  Pallas kernels  40.7 us (90%)
  between operations  2.33 us (5%)
  local copies, waits for them, and re-layouts  1.87 us (4%)
    pallas_call x1, Pallas kernels, shards(): pl.pallas_call(functools.partial(kernel, n, g), out_shape=(jax.ShapeDtype...  40.7 us
    unnamed x1, local copies, waits for them, and re-layouts  1.87 us

profile of v2, /device:TPU:0, one launch (start us, length us, event | category | flops | bytes accessed | tf_op | source)
XLA Modules:
  0.0 45.0 jit_solution(11114985118440604190)
XLA Ops:
  0.6 40.7 %shard_map.59 = (bf16[64,4096]{1,0:T(8,128)(2,1)}, f32[1]{0:T(128)}) custom-call(bf16[64,4096]{1,0:T(8,128)(2,1)} %bitcast.2, f32[64,4096]{1,0:T(8,128)} %vin_hbm.1, bf16[256,256]{1,0:T(8,128)(2,1)} %constant.4.clone.hx_hbm, bf16[512,512]{1,0:T(8,128)(2,1)} %constant.5.clone.hy_hbm), custom_call_target="tpu_custom_call" | custom-call | tf_op jit(solution)/shard_map/pallas_call | solution.py:247
  41.4 1.9 %copy.8 = bf16[1,64,4096]{2,1,0:T(8,128)(2,1)} copy(bf16[1,64,4096]{2,1,0:T(8,128)(2,1)} %bitcast.3) | data formatting | bytes 1048576
